TPU v7x, 32 devices: a whole 2x2x4 slice. The times are simulated.
32 devices in a mesh: grp: 1, tile: 16 (over z, x, core), mem: 2 (over y).
Axes of the slice: x: 2, y: 2, z: 4, core: 2. Of those that a mesh axis runs over, the one named last changes fastest.
Arguments:
- ens_coarse: bfloat16 [1, 80, 128, 64, 64], P('grp', 'mem', None, 'tile'), may hold values from -6 to 6
- col_interp: bfloat16 [128, 64], replicated, may hold values from -0.75 to 0.75
- row_weights: bfloat16 [3, 128], replicated, may hold values from 0.099609375 to 0.8984375
- ctrl_vec: float32 [1, 128, 128, 128], P('grp', None, 'tile'), may hold values from -24 to 24
- band_loc: bfloat16 [128, 24], P('tile'), may hold values from -1.25 to 1.25
- row_loc: bfloat16 [128, 128], replicated, may hold values from -0.5 to 0.5
- level_loc: bfloat16 [128, 128], replicated, may hold values from -0.5 to 0.5
- hx_pert: bfloat16 [1, 80, 65536], P('grp', None, ('tile', 'mem')), may hold values from -3 to 3
- innov: float32 [1, 65536], P('grp', ('tile', 'mem')), may hold values from -48 to 48
- obs_prec: float32 [1, 65536], P('grp', ('tile', 'mem')), may hold values from 0.3 to 3
- obs_region: int32 [1, 65536], P('grp', ('tile', 'mem')), may hold values from 0 to 7
Outputs:
- increment: float32 [1, 128, 128, 128], P('grp', 'mem', 'tile')
- letkf_weights: float32 [128, 80], P('tile')
Inputs may be any that keep to these rules, and one draw needn't show every extreme that they name: `obs_region`: the region of an observation among the 8 regions of its block of 4096 observations.
All inputs are finite; a program needn't handle non-finite values.
Results may differ from a plain program's by a relative error of at most 0.018.
Values may be sent and summed in bfloat16 or wider, within the bound.
A program may use at most 128 MiB of HBM per device.

v0:
```python
import jax
import jax.numpy as jnp
from jax import lax
from jax.sharding import PartitionSpec as P

NREG = 8


def extended(value, sides, width):
    for axis, dim in sides:
        peers, length = (lax.axis_size(axis), value.shape[dim])
        up = [(i, (i + 1) % peers) for i in range(peers - 1)]
        down = [(j, i) for i, j in up]
        last = lax.slice_in_dim(value, length - width, length, axis=dim)
        first = lax.slice_in_dim(value, 0, width, axis=dim)
        before = lax.ppermute(last, axis, up)
        after = lax.ppermute(first, axis, down)
        value = jnp.concatenate([before, value, after], axis=dim)
    return value


def row_matrix(row_weights, fine_rows, coarse_rows):
    fine_index = lax.broadcasted_iota(jnp.int32, (fine_rows, coarse_rows), 0)
    coarse_index = lax.broadcasted_iota(jnp.int32, (fine_rows, coarse_rows), 1)
    weights = row_weights.astype(jnp.float32)
    stencil = jnp.zeros((fine_rows, coarse_rows), jnp.float32)
    for offset in range(3):
        matched = coarse_index == fine_index // 2 + offset - 1
        stencil = stencil + jnp.where(matched, weights[offset][:, None], 0.0)
    return stencil.astype(jnp.bfloat16)


def solve_weights(gram_sums, right_side):
    member_count = gram_sums.shape[-1]
    system = gram_sums + (member_count - 1) * jnp.eye(member_count, dtype=jnp.float32)
    factor = jnp.linalg.cholesky(system)
    halfway = lax.linalg.triangular_solve(factor, right_side[..., None], left_side=True, lower=True)
    result = lax.linalg.triangular_solve(
        factor, halfway, left_side=True, lower=True, transpose_a=True
    )
    return result[..., 0]


def body(
    ens_coarse,
    col_interp,
    row_weights,
    ctrl_vec,
    band_loc,
    row_loc,
    level_loc,
    hx_pert,
    innov,
    obs_prec,
    obs_region,
):
    fine_rows = row_weights.shape[1]
    columns = band_loc.shape[0]
    total_members = hx_pert.shape[1]
    observed = hx_pert[0]
    weighted = (observed * obs_prec[0][None, :]).astype(jnp.bfloat16)
    labels = lax.broadcasted_iota(jnp.int32, (NREG, observed.shape[1]), 0)
    member_of = obs_region[0][None, :] == labels
    masked = jnp.where(member_of[:, None, :], weighted[None], jnp.zeros((), jnp.bfloat16))
    gram_sums = jnp.einsum("rko,jo->rkj", masked, observed, preferred_element_type=jnp.float32)
    innov_rows = jnp.where(member_of, innov[0][None, :], 0.0)
    right_side = jnp.dot(
        innov_rows, weighted.astype(jnp.float32).T, precision=lax.Precision.HIGHEST
    )
    gram_sums, right_side = lax.psum((gram_sums, right_side), ("grp", "mem"))
    coarse_cols = jnp.einsum(
        "tklic,jc->tklij", ens_coarse, col_interp, preferred_element_type=jnp.float32
    ).astype(jnp.bfloat16)
    stencil = row_matrix(row_weights, fine_rows, fine_rows // 2)
    refined = jnp.einsum(
        "tklij,ri->tkljr",
        lax.all_to_all(coarse_cols, "tile", split_axis=4, concat_axis=3, tiled=True),
        stencil,
        preferred_element_type=jnp.float32,
    ).astype(jnp.bfloat16)
    member_fine = refined[0]
    slot_term = member_fine * ctrl_vec[0][None]
    projected = lax.psum(slot_term.astype(jnp.bfloat16), "grp")
    padded = extended(projected, (("tile", 2),), columns)
    banded = jnp.einsum(
        "jq,klqr->kljr", band_loc, padded, preferred_element_type=jnp.float32
    ).astype(jnp.bfloat16)
    row_mixed = jnp.einsum(
        "kljs,rs->kljr", banded, row_loc, preferred_element_type=jnp.float32
    ).astype(jnp.bfloat16)
    localized = jnp.einsum(
        "lm,kmjr->kljr", level_loc, row_mixed, preferred_element_type=jnp.float32
    ).astype(jnp.bfloat16)
    increment = lax.psum_scatter(
        jnp.sum(member_fine.astype(jnp.float32) * localized.astype(jnp.float32), axis=0),
        "mem",
        scatter_dimension=0,
        tiled=True,
    ) / (total_members - 1)
    per_device = NREG // lax.axis_size("mem")
    first_region = lax.axis_index("mem") * per_device
    own_weights = solve_weights(
        lax.dynamic_slice_in_dim(gram_sums, first_region, per_device, 0),
        lax.dynamic_slice_in_dim(right_side, first_region, per_device, 0),
    )
    weights = lax.all_gather(own_weights, "mem", axis=0, tiled=True)
    return (increment[None], weights)


def solution(mesh):
    placed = (
        P("grp", "mem", None, "tile", None),
        P(),
        P(),
        P("grp", None, "tile", None),
        P("tile", None),
        P(),
        P(),
        P("grp", None, ("tile", "mem")),
        P("grp", ("tile", "mem")),
        P("grp", ("tile", "mem")),
        P("grp", ("tile", "mem")),
    )
    return jax.shard_map(
        body,
        mesh=mesh,
        in_specs=placed,
        out_specs=(P("grp", "mem", "tile", None), P("tile", None)),
        check_vma=False,
    )
```

profile of v0, /device:TPU:14, one launch (start us, length us, event | category | flops | bytes accessed | tf_op | source)
XLA Modules:
  0.0 528.6 jit_solution(12089126773845195729)
XLA Ops:
  7.2 1.7 copy-done
  8.9 4.1 convert_bitcast_fusion
  13.0 9.7 %copy.37 = bf16[1,40,128,4,128]{2,3,1,0,4:T(4,128)(2,1)} copy(bf16[1,40,128,4,128]{4,2,3,1,0:T(8,128)(2,1)} %convert_bitcast_fusion) | data formatting | bytes 10485760 | tf_op jit(solution)/shard_map/convert_element_type | solution.py:73
  22.7 6.2 %all-to-all-start = ((bf16[1,40,128,4,128]{2,3,1,0,4:T(4,128)(2,1)}), bf16[1,40,128,4,128]{2,3,1,0,4:T(4,128)(2,1)}, u32[]{:S(2)}, u32[]{:S(2)}) async-start(bf16[1,40,128,4,128]{2,3,1,0,4:T(4,128)(2,1)} %copy.37), calls=%async_computation | async-start | bytes 10485760 | tf_op jit(solution)/shard_map/all_to_all | solution.py:77
  29.2 114.4 %all-to-all-done = bf16[1,40,128,4,128]{2,3,1,0,4:T(4,128)(2,1)} async-done(((bf16[1,40,128,4,128]{2,3,1,0,4:T(4,128)(2,1)}), bf16[1,40,128,4,128]{2,3,1,0,4:T(4,128)(2,1)}, u32[]{:S(2)}, u32[]{:S(2)}) %all-to-all-start) | async-done | bytes 5242912 | tf_op jit(solution)/shard_map/all_to_all | solution.py:77
  143.6 4.5 copy.72
  148.1 5.1 copy.39
  153.3 8.6 %fusion.2 = (bf16[40,128,8,128]{3,1,2,0:T(8,128)(2,1)}, bf16[40,128,8,128]{3,1,2,0:T(8,128)(2,1)}) fusion(f32[128,8,128]{2,0,1:T(8,128)S(1)} %copy.40, bf16[40,128,64,8]{1,2,3,0:T(8,128)(2,1)S(1)} %bitcast.96, f32[128]{0:T(128)S(1)} %get-tuple-element.7, f32[128]{0:T(128)S(1)} %get-tuple-element.8, f32[128]{0:T(128)S(1)} %get-tuple-element.6, ...), kind=kOutput, calls=%fused_computation.5 | convolution fusion | flops 692158464 | bytes 26741376 | tf_op jit(solution)/shard_map/tklij,ri->tkljr/dot_general | solution.py:75
  161.9 1.9 collective-permute-start.1
  163.8 2.4 collective-permute-start
  166.3 1.9 fusion.21
  168.8 4.9 psum.18
  173.8 21.8 %all-reduce.2.cloned.1.call-done = f32[8,80,80]{1,2,0:T(8,128)} async-done(((f32[8,80,80]{1,2,0:T(8,128)}), f32[8,80,80]{1,2,0:T(8,128)}) %all-reduce.2.cloned.1.call-update) | async-done | bytes 204816 | tf_op jit(solution)/shard_map/psum | solution.py:70
  195.6 0.9 dynamic-slice_add_fusion
  196.7 193.2 %collective-permute-done.1 = bf16[40,128,8,128]{3,1,2,0:T(8,128)(2,1)} collective-permute-done((bf16[40,128,8,128]{3,1,2,0:T(8,128)(2,1)}, bf16[40,128,8,128]{3,1,2,0:T(8,128)(2,1)}, u32[]{:S(2)}, u32[]{:S(2)}) %collective-permute-start.1) | collective-permute-done | bytes 10485792 | tf_op jit(solution)/shard_map/ppermute | solution.py:17
  389.9 3.4 collective-permute-done
  393.3 21.7 %pad_maximum_fusion = bf16[40,128,24,128]{3,1,2,0:T(8,128)(2,1)} fusion(bf16[40,128,8,128]{3,1,2,0:T(8,128)(2,1)} %collective-permute-done.1, bf16[40,128,8,128]{3,1,2,0:T(8,128)(2,1)} %get-tuple-element.9, bf16[40,128,8,128]{3,1,2,0:T(8,128)(2,1)} %collective-permute-done), kind=kLoop, calls=%fused_computation | loop fusion | flops 31457280 | bytes 62914560 | tf_op jit(solution)/shard_map/concatenate | solution.py:18
  415.0 32.5 %fusion.15 = bf16[40,128,8,128]{3,2,1,0:T(8,128)(2,1)} fusion(bf16[40,128,24,128]{3,1,2,0:T(8,128)(2,1)} %pad_maximum_fusion, bf16[128,128]{1,0:T(8,128)(2,1)S(1)} %copy-done.5, bf16[8,24]{1,0:T(8,128)(2,1)S(1)} %copy-done.8), kind=kOutput, calls=%fused_computation.13 | convolution fusion | flops 1604321280 | bytes 41976192 | tf_op jit(solution)/shard_map/kljs,rs->kljr/dot_general | solution.py:88
  447.6 12.5 %fusion.3 = f32[128,8,128]{2,0,1:T(8,128)} fusion(bf16[40,128,8,128]{3,1,2,0:T(8,128)(2,1)} %get-tuple-element.10, bf16[40,128,8,128]{3,2,1,0:T(8,128)(2,1)} %fusion.15, bf16[128,128]{1,0:T(8,128)(2,1)S(1)} %copy-done.10), kind=kOutput, calls=%fused_computation.6 | convolution fusion | flops 1368260608 | bytes 21528576 | tf_op jit(solution)/shard_map/lm,kmjr->kljr/dot_general | solution.py:91
  460.2 29.3 %custom-call.9 = f32[4,80,80]{2,1,0:T(8,128)S(1)} custom-call(f32[4,80,80]{2,1,0:T(8,128)S(1)} %fusion.34), custom_call_target="Cholesky" | custom-call | tf_op jit(solution)/shard_map/jit(cholesky)/cholesky | solution.py:36
  489.7 24.6 %custom-call.10 = f32[4,1,80,80]{2,3,1,0:T(8,128)S(1)} custom-call(f32[4,1,80,80]{3,2,1,0:T(8,128)S(1)} %select_bitcast_fusion), custom_call_target="InvertDiagBlocksLowerTriangular" | custom-call | tf_op jit(solution)/shard_map/triangular_solve | solution.py:38
  515.0 4.4 all-gather
  519.3 1.0 multiply_bitcast_fusion
  520.3 0.9 copy.47
  (49 shorter events, 2.4 us)
Async XLA Ops:
  7.2 1.7 copy-start
  13.0 16.0 %copy-start.2 = (f32[1,128,8,128]{3,2,1,0:T(8,128)S(1)}, f32[1,128,8,128]{3,2,1,0:T(8,128)}, u32[]{:S(2)}) copy-start(f32[1,128,8,128]{3,2,1,0:T(8,128)} %param.14) | copy-start | bytes 1572868
  13.0 16.1 %copy-start.9 = (bf16[3,128]{1,0:T(4,128)(2,1)S(1)}, bf16[3,128]{1,0:T(4,128)(2,1)}, u32[]{:S(2)}) copy-start(bf16[3,128]{1,0:T(4,128)(2,1)} %param.13) | copy-start | bytes 2308
  22.7 120.9 %all-to-all-start = ((bf16[1,40,128,4,128]{2,3,1,0,4:T(4,128)(2,1)}), bf16[1,40,128,4,128]{2,3,1,0,4:T(4,128)(2,1)}, u32[]{:S(2)}, u32[]{:S(2)}) async-start(bf16[1,40,128,4,128]{2,3,1,0,4:T(4,128)(2,1)} %copy.37), calls=%async_computation | async-start | bytes 10485760 | tf_op jit(solution)/shard_map/all_to_all | solution.py:77
  29.0 166.6 %all-reduce.2.cloned.1.call-start = ((), (), s32[]{:S(2)}) async-start(), calls=%async_computation.3 | async-start | bytes 655360 | tf_op jit(solution)/shard_map/psum | solution.py:70
  153.2 13.0 %copy-start.6 = (s32[1,2048]{1,0:T(1,128)S(1)}, s32[1,2048]{1,0:T(1,128)}, u32[]{:S(2)}) copy-start(s32[1,2048]{1,0:T(1,128)} %param.21) | copy-start | bytes 24580
  153.2 13.0 %copy-start.4 = (bf16[1,80,2048]{2,1,0:T(8,128)(2,1)S(1)}, bf16[1,80,2048]{2,1,0:T(8,128)(2,1)}, u32[]{:S(2)}) copy-start(bf16[1,80,2048]{2,1,0:T(8,128)(2,1)} %param.18) | copy-start | bytes 983044
  153.2 13.0 %copy-start.7 = (f32[1,2048]{1,0:T(1,128)S(1)}, f32[1,2048]{1,0:T(1,128)}, u32[]{:S(2)}) copy-start(f32[1,2048]{1,0:T(1,128)} %param.20) | copy-start | bytes 24580
  153.3 15.2 %copy-start.11 = (f32[1,2048]{1,0:T(1,128)S(1)}, f32[1,2048]{1,0:T(1,128)}, u32[]{:S(2)}) copy-start(f32[1,2048]{1,0:T(1,128)} %param.19) | copy-start | bytes 24580
  161.9 228.0 %collective-permute-start.1 = (bf16[40,128,8,128]{3,1,2,0:T(8,128)(2,1)}, bf16[40,128,8,128]{3,1,2,0:T(8,128)(2,1)}, u32[]{:S(2)}, u32[]{:S(2)}) collective-permute-start(bf16[40,128,8,128]{3,1,2,0:T(8,128)(2,1)} %get-tuple-element.9), channel_id=1, source_target_pairs={{2,0},{4,2},{6,4},{8,6},{10,8},{12,10},{14,12},{16,14},{18,16},{20... | collective-permute-start | bytes 31457288 | tf_op jit(solution)/shard_map/ppermute | solution.py:17
  163.8 229.5 %collective-permute-start = (bf16[40,128,8,128]{3,1,2,0:T(8,128)(2,1)}, bf16[40,128,8,128]{3,1,2,0:T(8,128)(2,1)}, u32[]{:S(2)}, u32[]{:S(2)}) collective-permute-start(bf16[40,128,8,128]{3,1,2,0:T(8,128)(2,1)} %get-tuple-element.9), channel_id=1, source_target_pairs={{0,2},{2,4},{4,6},{6,8},{8,10},{10,12},{12,14},{14,16},{16,18},{18... | collective-permute-start | bytes 31457288 | tf_op jit(solution)/shard_map/ppermute | solution.py:16
  168.3 351.0 %reduce-scatter.2.cloned.1.call-start = ((), (), s32[]{:S(2)}) async-start(), calls=%async_computation.2 | async-start | bytes 786432 | tf_op jit(solution)/shard_map/reduce_scatter | solution.py:94
  196.6 218.4 %copy-start.5 = (bf16[128,128]{1,0:T(8,128)(2,1)S(1)}, bf16[128,128]{1,0:T(8,128)(2,1)}, u32[]{:S(2)}) copy-start(bf16[128,128]{1,0:T(8,128)(2,1)} %param.16) | copy-start | bytes 98308
  196.7 218.4 %copy-start.8 = (bf16[8,24]{1,0:T(8,128)(2,1)S(1)}, bf16[8,24]{1,0:T(8,128)(2,1)}, u32[]{:S(2)}) copy-start(bf16[8,24]{1,0:T(8,128)(2,1)} %param.15) | copy-start | bytes 1156
  415.0 32.5 %copy-start.10 = (bf16[128,128]{1,0:T(8,128)(2,1)S(1)}, bf16[128,128]{1,0:T(8,128)(2,1)}, u32[]{:S(2)}) copy-start(bf16[128,128]{1,0:T(8,128)(2,1)} %param.17) | copy-start | bytes 98308
  447.6 74.2 %copy-start.1 = (bf16[1,40,128,4,64]{2,4,3,1,0:T(8,128)(2,1)S(1)}, bf16[1,40,128,4,64]{2,4,3,1,0:T(8,128)(2,1)}, u32[]{:S(2)}) copy-start(bf16[1,40,128,4,64]{2,4,3,1,0:T(8,128)(2,1)} %param.11) | copy-start | bytes 7864324
  447.6 12.5 %copy-start.3 = (f32[8,80,80]{1,2,0:T(8,128)S(1)}, f32[8,80,80]{1,2,0:T(8,128)}, u32[]{:S(2)}) copy-start(f32[8,80,80]{1,2,0:T(8,128)} %all-reduce.2.cloned.1.call-done) | copy-start | bytes 614404
Sparse Core Ops, SparseCore 0:
  168.4 27.1 all-reduce.1
  460.2 12.7 reduce-scatter.1
where the time goes:
time: 529 us
  waiting for transfers between devices  333 us (63%)
  other arithmetic  78 us (15%)
  matrix products  60.6 us (11%)
  local copies, waits for them, and re-layouts  22.9 us (4%)
  between operations  14.3 us (3%)
  starting transfers between devices  10.6 us (2%)
  blocking collectives  9.32 us (2%)
    ppermute x1, waiting for transfers between devices, extended(): after = lax.ppermute(first, axis, down)  193 us
    all_to_all x1, waiting for transfers between devices, body(): lax.all_to_all(coarse_cols, 'tile', split_axis=4, concat_axis=3, tiled=True)  114 us
    dot_general x1, matrix products, body(): jnp.einsum('kljs,rs->kljr', banded, row_loc, preferred_element_type=jnp.f...  32.5 us
    another operation x4, other arithmetic, solve_weights(): factor = jnp.linalg.cholesky(system)  29.5 us
    another operation x3, other arithmetic, solve_weights(): lax.linalg.triangular_solve(factor, halfway, left_side=True, lower=True,...  24.7 us
    psum x1, waiting for transfers between devices, body(): gram_sums, right_side = lax.psum((gram_sums, right_side), ('grp', 'mem'))  21.8 us
    concatenate x1, other arithmetic, extended(): value = jnp.concatenate([before, value, after], axis=dim)  21.7 us
    dot_general x1, matrix products, body(): jnp.einsum('lm,kmjr->kljr', level_loc, row_mixed, preferred_element_type=...  12.5 us
  transfers between devices with their start and end apart: 5, of which 4 were waited for; matrix products, arithmetic and copies ran while one was open for 11% of the time, Pallas kernels for 0%

commit v1 on v0

--- a/solution.py
+++ b/solution.py
@@ -17,6 +17,33 @@
         after = lax.ppermute(first, axis, down)
         value = jnp.concatenate([before, value, after], axis=dim)
     return value
+
+
+def swap_add(value):
+    peers = lax.axis_size("mem")
+    me = lax.axis_index("mem")
+    length = value.shape[0] // peers
+    total = lax.dynamic_slice_in_dim(value, me * length, length, 0)
+    for shift in range(1, peers):
+        other = lax.rem(me + shift, peers)
+        part = lax.dynamic_slice_in_dim(value, other * length, length, 0)
+        pairs = [(i, (i + shift) % peers) for i in range(peers)]
+        total = total + lax.ppermute(part, "mem", pairs)
+    return total
+
+
+def collect(value):
+    peers = lax.axis_size("mem")
+    me = lax.axis_index("mem")
+    length = value.shape[0]
+    result = jnp.zeros((peers * length,) + value.shape[1:], value.dtype)
+    result = lax.dynamic_update_slice_in_dim(result, value, me * length, 0)
+    for shift in range(1, peers):
+        pairs = [(i, (i + shift) % peers) for i in range(peers)]
+        moved = lax.ppermute(value, "mem", pairs)
+        source = lax.rem(me + peers - shift, peers)
+        result = lax.dynamic_update_slice_in_dim(result, moved, source * length, 0)
+    return result
 
 
 def row_matrix(row_weights, fine_rows, coarse_rows):
@@ -67,7 +94,8 @@
     right_side = jnp.dot(
         innov_rows, weighted.astype(jnp.float32).T, precision=lax.Precision.HIGHEST
     )
-    gram_sums, right_side = lax.psum((gram_sums, right_side), ("grp", "mem"))
+    sums = jnp.concatenate([gram_sums, right_side[:, :, None]], axis=2)
+    sums = swap_add(lax.psum(sums, "grp") if lax.axis_size("grp") > 1 else sums)
     coarse_cols = jnp.einsum(
         "tklic,jc->tklij", ens_coarse, col_interp, preferred_element_type=jnp.float32
     ).astype(jnp.bfloat16)
@@ -80,7 +108,9 @@
     ).astype(jnp.bfloat16)
     member_fine = refined[0]
     slot_term = member_fine * ctrl_vec[0][None]
-    projected = lax.psum(slot_term.astype(jnp.bfloat16), "grp")
+    projected = slot_term.astype(jnp.bfloat16)
+    if lax.axis_size("grp") > 1:
+        projected = lax.psum(projected, "grp")
     padded = extended(projected, (("tile", 2),), columns)
     banded = jnp.einsum(
         "jq,klqr->kljr", band_loc, padded, preferred_element_type=jnp.float32
@@ -91,19 +121,11 @@
     localized = jnp.einsum(
         "lm,kmjr->kljr", level_loc, row_mixed, preferred_element_type=jnp.float32
     ).astype(jnp.bfloat16)
-    increment = lax.psum_scatter(
-        jnp.sum(member_fine.astype(jnp.float32) * localized.astype(jnp.float32), axis=0),
-        "mem",
-        scatter_dimension=0,
-        tiled=True,
+    increment = swap_add(
+        jnp.sum(member_fine.astype(jnp.float32) * localized.astype(jnp.float32), axis=0)
     ) / (total_members - 1)
-    per_device = NREG // lax.axis_size("mem")
-    first_region = lax.axis_index("mem") * per_device
-    own_weights = solve_weights(
-        lax.dynamic_slice_in_dim(gram_sums, first_region, per_device, 0),
-        lax.dynamic_slice_in_dim(right_side, first_region, per_device, 0),
-    )
-    weights = lax.all_gather(own_weights, "mem", axis=0, tiled=True)
+    own_weights = solve_weights(sums[:, :, :total_members], sums[:, :, total_members])
+    weights = collect(own_weights)
     return (increment[None], weights)
 
 

time: 529 us -> 461 us (0.87)
  waiting for transfers between devices: 333 us -> 288 us
  between operations: 14.3 us -> 0.94 us
  blocking collectives: 9.32 us -> 0 us
    ppermute x1, waiting for transfers between devices: 193 us -> 161 us  [extended(): after = lax.ppermute(first, axis, down)]
    psum x1 -> x0, waiting for transfers between devices: 21.8 us -> none  [body(): gram_sums, right_side = lax.psum((gram_sums, right_side), ('grp', 'mem'))]
    ppermute x0 -> x3, waiting for transfers between devices: none -> 9.2 us  [the longest x2 5.22 us: swap_add(): total = total + lax.ppermute(part, 'mem', pairs)]
  transfers between devices with their start and end apart: 5 -> 6, of which waited for: 4 -> 5; matrix products, arithmetic and copies ran while one was open for 11% -> 12% of each run, Pallas kernels for 0% -> 0%
where the time goes in v1:
time: 461 us; the launch traced here: 460 us
  waiting for transfers between devices  288 us (62%)
  other arithmetic  76.2 us (17%)
  matrix products  59.2 us (13%)
  local copies, waits for them, and re-layouts  22.4 us (5%)
  starting transfers between devices  13.4 us (3%)
    ppermute x1, waiting for transfers between devices, extended(): after = lax.ppermute(first, axis, down)  161 us
    all_to_all x1, waiting for transfers between devices, body(): lax.all_to_all(coarse_cols, 'tile', split_axis=4, concat_axis=3, tiled=True)  114 us
    dot_general x1, matrix products, body(): jnp.einsum('kljs,rs->kljr', banded, row_loc, preferred_element_type=jnp.f...  32.5 us
    another operation x4, other arithmetic, solve_weights(): factor = jnp.linalg.cholesky(system)  29.5 us
    another operation x3, other arithmetic, solve_weights(): lax.linalg.triangular_solve(factor, halfway, left_side=True, lower=True,...  24.7 us
    concatenate x1, other arithmetic, extended(): value = jnp.concatenate([before, value, after], axis=dim)  21.7 us
    dot_general x1, matrix products, body(): jnp.einsum('lm,kmjr->kljr', level_loc, row_mixed, preferred_element_type=...  11.8 us
    convert_element_type x1, local copies, waits for them, and re-layouts, body(): coarse_cols = jnp.einsum('tklic,jc->tklij', ens_coarse, col_interp, prefe...  9.82 us
  transfers between devices with their start and end apart: 6, of which 5 were waited for; matrix products, arithmetic and copies ran while one was open for 12% of the time, Pallas kernels for 0%

profile of v1, /device:TPU:14, one launch (start us, length us, event | category | flops | bytes accessed | tf_op | source)
XLA Modules:
  0.0 460.4 jit_solution(12069785999459660536)
XLA Ops:
  0.6 1.7 copy-done
  2.4 4.1 convert_bitcast_fusion
  6.5 9.8 %copy.37 = bf16[1,40,128,4,128]{2,3,1,0,4:T(4,128)(2,1)} copy(bf16[1,40,128,4,128]{4,2,3,1,0:T(8,128)(2,1)} %convert_bitcast_fusion) | data formatting | bytes 10485760 | tf_op jit(solution)/shard_map/convert_element_type | solution.py:101
  16.3 6.2 %all-to-all-start = ((bf16[1,40,128,4,128]{2,3,1,0,4:T(4,128)(2,1)}), bf16[1,40,128,4,128]{2,3,1,0,4:T(4,128)(2,1)}, u32[]{:S(2)}, u32[]{:S(2)}) async-start(bf16[1,40,128,4,128]{2,3,1,0,4:T(4,128)(2,1)} %copy.37), calls=%async_computation | async-start | bytes 10485760 | tf_op jit(solution)/shard_map/all_to_all | solution.py:105
  22.7 114.5 %all-to-all-done = bf16[1,40,128,4,128]{2,3,1,0,4:T(4,128)(2,1)} async-done(((bf16[1,40,128,4,128]{2,3,1,0,4:T(4,128)(2,1)}), bf16[1,40,128,4,128]{2,3,1,0,4:T(4,128)(2,1)}, u32[]{:S(2)}, u32[]{:S(2)}) %all-to-all-start) | async-done | bytes 5242912 | tf_op jit(solution)/shard_map/all_to_all | solution.py:105
  137.2 4.5 copy.72
  141.7 5.1 %copy.39 = bf16[1,40,128,16,4,8]{2,4,3,5,1,0:T(4,128)(2,1)S(1)} copy(bf16[1,40,128,16,4,8]{2,5,3,4,1,0:T(8,128)(2,1)S(1)} %bitcast.94) | data formatting | bytes 10485760 | tf_op jit(solution)/shard_map/all_to_all | solution.py:105
  146.8 8.6 %fusion.2 = (bf16[40,128,8,128]{3,1,2,0:T(8,128)(2,1)}, bf16[40,128,8,128]{3,1,2,0:T(8,128)(2,1)}) fusion(f32[128,8,128]{2,0,1:T(8,128)S(1)} %copy.40, bf16[40,128,64,8]{1,2,3,0:T(8,128)(2,1)S(1)} %bitcast.95, f32[128]{0:T(128)S(1)} %get-tuple-element.7, f32[128]{0:T(128)S(1)} %get-tuple-element.8, f32[128]{0:T(128)S(1)} %get-tuple-element.6, ...), kind=kOutput, calls=%fused_computation.5 | convolution fusion | flops 692158464 | bytes 26741376 | tf_op jit(solution)/shard_map/tklij,ri->tkljr/dot_general | solution.py:103
  155.4 1.9 collective-permute-start.1
  157.4 2.6 collective-permute-start
  160.5 1.2 fusion.21
  161.7 0.6 collective-permute-start.3
  162.4 5.2 %collective-permute-done.3 = f32[4,80,81]{1,2,0:T(8,128)S(1)} collective-permute-done((f32[4,80,81]{1,2,0:T(8,128)S(1)}, f32[4,80,81]{1,2,0:T(8,128)S(1)}, u32[]{:S(2)}, u32[]{:S(2)}) %collective-permute-start.3) | collective-permute-done | bytes 103712 | tf_op jit(solution)/shard_map/ppermute | solution.py:31
  167.8 29.3 %custom-call.9 = f32[4,80,80]{2,1,0:T(8,128)S(1)} custom-call(f32[4,80,80]{2,1,0:T(8,128)S(1)} %fusion.37), custom_call_target="Cholesky" | custom-call | tf_op jit(solution)/shard_map/jit(cholesky)/cholesky | solution.py:63
  197.4 24.6 %custom-call.10 = f32[4,1,80,80]{2,3,1,0:T(8,128)S(1)} custom-call(f32[4,1,80,80]{3,2,1,0:T(8,128)S(1)} %select_bitcast_fusion), custom_call_target="InvertDiagBlocksLowerTriangular" | custom-call | tf_op jit(solution)/shard_map/triangular_solve | solution.py:65
  222.3 161.2 %collective-permute-done.1 = bf16[40,128,8,128]{3,1,2,0:T(8,128)(2,1)} collective-permute-done((bf16[40,128,8,128]{3,1,2,0:T(8,128)(2,1)}, bf16[40,128,8,128]{3,1,2,0:T(8,128)(2,1)}, u32[]{:S(2)}, u32[]{:S(2)}) %collective-permute-start.1) | collective-permute-done | bytes 10485792 | tf_op jit(solution)/shard_map/ppermute | solution.py:17
  383.4 3.4 collective-permute-done
  386.8 21.7 %pad_maximum_fusion = bf16[40,128,24,128]{3,1,2,0:T(8,128)(2,1)} fusion(bf16[40,128,8,128]{3,1,2,0:T(8,128)(2,1)} %collective-permute-done.1, bf16[40,128,8,128]{3,1,2,0:T(8,128)(2,1)} %get-tuple-element.9, bf16[40,128,8,128]{3,1,2,0:T(8,128)(2,1)} %collective-permute-done), kind=kLoop, calls=%fused_computation | loop fusion | flops 31457280 | bytes 62914560 | tf_op jit(solution)/shard_map/concatenate | solution.py:18
  408.6 32.5 %fusion.15 = bf16[40,128,8,128]{3,2,1,0:T(8,128)(2,1)} fusion(bf16[40,128,24,128]{3,1,2,0:T(8,128)(2,1)} %pad_maximum_fusion, bf16[128,128]{1,0:T(8,128)(2,1)S(1)} %copy-done.4, bf16[8,24]{1,0:T(8,128)(2,1)S(1)} %copy-done.8), kind=kOutput, calls=%fused_computation.13 | convolution fusion | flops 1604321280 | bytes 41976192 | tf_op jit(solution)/shard_map/kljs,rs->kljr/dot_general | solution.py:118
  441.1 11.8 %fusion.3 = f32[128,8,128]{2,0,1:T(8,128)S(1)} fusion(bf16[40,128,8,128]{3,1,2,0:T(8,128)(2,1)} %get-tuple-element.10, bf16[40,128,8,128]{3,2,1,0:T(8,128)(2,1)} %fusion.15, bf16[128,128]{1,0:T(8,128)(2,1)S(1)} %copy-done.10), kind=kOutput, calls=%fused_computation.6 | convolution fusion | flops 1368260608 | bytes 21528576 | tf_op jit(solution)/shard_map/lm,kmjr->kljr/dot_general | solution.py:121
  453.0 0.6 collective-permute-start.2
  453.9 1.5 collective-permute-start.4
  455.5 4.0 collective-permute-done.4
  459.5 0.9 copy.47
  (51 shorter events, 1.9 us)
Async XLA Ops:
  0.6 1.7 copy-start
  6.5 16.1 %copy-start.2 = (f32[1,128,8,128]{3,2,1,0:T(8,128)S(1)}, f32[1,128,8,128]{3,2,1,0:T(8,128)}, u32[]{:S(2)}) copy-start(f32[1,128,8,128]{3,2,1,0:T(8,128)} %param.14) | copy-start | bytes 1572868
  6.5 16.2 %copy-start.9 = (bf16[3,128]{1,0:T(4,128)(2,1)S(1)}, bf16[3,128]{1,0:T(4,128)(2,1)}, u32[]{:S(2)}) copy-start(bf16[3,128]{1,0:T(4,128)(2,1)} %param.13) | copy-start | bytes 2308
  16.3 120.9 %all-to-all-start = ((bf16[1,40,128,4,128]{2,3,1,0,4:T(4,128)(2,1)}), bf16[1,40,128,4,128]{2,3,1,0,4:T(4,128)(2,1)}, u32[]{:S(2)}, u32[]{:S(2)}) async-start(bf16[1,40,128,4,128]{2,3,1,0,4:T(4,128)(2,1)} %copy.37), calls=%async_computation | async-start | bytes 10485760 | tf_op jit(solution)/shard_map/all_to_all | solution.py:105
  146.8 13.2 %copy-start.3 = (bf16[1,80,2048]{2,1,0:T(8,128)(2,1)S(1)}, bf16[1,80,2048]{2,1,0:T(8,128)(2,1)}, u32[]{:S(2)}) copy-start(bf16[1,80,2048]{2,1,0:T(8,128)(2,1)} %param.18) | copy-start | bytes 983044
  146.8 13.2 %copy-start.5 = (s32[1,2048]{1,0:T(1,128)S(1)}, s32[1,2048]{1,0:T(1,128)}, u32[]{:S(2)}) copy-start(s32[1,2048]{1,0:T(1,128)} %param.21) | copy-start | bytes 24580
  146.8 13.2 %copy-start.6 = (f32[1,2048]{1,0:T(1,128)S(1)}, f32[1,2048]{1,0:T(1,128)}, u32[]{:S(2)}) copy-start(f32[1,2048]{1,0:T(1,128)} %param.20) | copy-start | bytes 24580
  146.8 13.2 %copy-start.11 = (f32[1,2048]{1,0:T(1,128)S(1)}, f32[1,2048]{1,0:T(1,128)}, u32[]{:S(2)}) copy-start(f32[1,2048]{1,0:T(1,128)} %param.19) | copy-start | bytes 24580
  155.4 228.0 %collective-permute-start.1 = (bf16[40,128,8,128]{3,1,2,0:T(8,128)(2,1)}, bf16[40,128,8,128]{3,1,2,0:T(8,128)(2,1)}, u32[]{:S(2)}, u32[]{:S(2)}) collective-permute-start(bf16[40,128,8,128]{3,1,2,0:T(8,128)(2,1)} %get-tuple-element.9), channel_id=1, source_target_pairs={{2,0},{4,2},{6,4},{8,6},{10,8},{12,10},{14,12},{16,14},{18,16},{20... | collective-permute-start | bytes 31457288 | tf_op jit(solution)/shard_map/ppermute | solution.py:17
  157.4 229.5 %collective-permute-start = (bf16[40,128,8,128]{3,1,2,0:T(8,128)(2,1)}, bf16[40,128,8,128]{3,1,2,0:T(8,128)(2,1)}, u32[]{:S(2)}, u32[]{:S(2)}) collective-permute-start(bf16[40,128,8,128]{3,1,2,0:T(8,128)(2,1)} %get-tuple-element.9), channel_id=1, source_target_pairs={{0,2},{2,4},{4,6},{6,8},{8,10},{10,12},{12,14},{14,16},{16,18},{18... | collective-permute-start | bytes 31457288 | tf_op jit(solution)/shard_map/ppermute | solution.py:16
  161.7 5.9 %collective-permute-start.3 = (f32[4,80,81]{1,2,0:T(8,128)S(1)}, f32[4,80,81]{1,2,0:T(8,128)S(1)}, u32[]{:S(2)}, u32[]{:S(2)}) collective-permute-start(f32[4,80,81]{1,2,0:T(8,128)S(1)} %fusion.31), channel_id=1, source_target_pairs={{0,1},{1,0},{2,3},{3,2},{4,5},{5,4},{6,7},{7,6},{8,9},{9,8},{10,11... | collective-permute-start | bytes 311048 | tf_op jit(solution)/shard_map/ppermute | solution.py:31
  222.3 186.3 %copy-start.4 = (bf16[128,128]{1,0:T(8,128)(2,1)S(1)}, bf16[128,128]{1,0:T(8,128)(2,1)}, u32[]{:S(2)}) copy-start(bf16[128,128]{1,0:T(8,128)(2,1)} %param.16) | copy-start | bytes 98308
  222.3 186.3 %copy-start.8 = (bf16[8,24]{1,0:T(8,128)(2,1)S(1)}, bf16[8,24]{1,0:T(8,128)(2,1)}, u32[]{:S(2)}) copy-start(bf16[8,24]{1,0:T(8,128)(2,1)} %param.15) | copy-start | bytes 1156
  408.6 32.5 %copy-start.10 = (bf16[128,128]{1,0:T(8,128)(2,1)S(1)}, bf16[128,128]{1,0:T(8,128)(2,1)}, u32[]{:S(2)}) copy-start(bf16[128,128]{1,0:T(8,128)(2,1)} %param.17) | copy-start | bytes 98308
  441.1 19.3 %copy-start.1 = (bf16[1,40,128,4,64]{2,4,3,1,0:T(8,128)(2,1)S(1)}, bf16[1,40,128,4,64]{2,4,3,1,0:T(8,128)(2,1)}, u32[]{:S(2)}) copy-start(bf16[1,40,128,4,64]{2,4,3,1,0:T(8,128)(2,1)} %param.11) | copy-start | bytes 7864324
  453.0 6.5 %collective-permute-start.2 = (f32[64,8,128]{2,0,1:T(8,128)S(1)}, f32[64,8,128]{2,0,1:T(8,128)S(1)}, u32[]{:S(2)}, u32[]{:S(2)}) collective-permute-start(f32[64,8,128]{2,0,1:T(8,128)S(1)} %constant_dynamic-slice_fusion), channel_id=1, source_target_pairs={{0,1},{1,0},{2,3},{3,2},{4,5},{5,4},{6,7},{7,6},{8,9},{9,8},{10,11... | collective-permute-start | bytes 786440 | tf_op jit(solution)/shard_map/ppermute | solution.py:31
  453.9 5.5 %collective-permute-start.4 = (f32[4,80]{1,0:T(4,128)S(1)}, f32[4,80]{1,0:T(4,128)S(1)}, u32[]{:S(2)}, u32[]{:S(2)}) collective-permute-start(f32[4,80]{1,0:T(4,128)S(1)} %bitcast.99), channel_id=1, source_target_pairs={{0,1},{1,0},{2,3},{3,2},{4,5},{5,4},{6,7},{7,6},{8,9},{9,8},{10,11... | collective-permute-start | bytes 3848 | tf_op jit(solution)/shard_map/ppermute | solution.py:43
  459.5 0.9 copy-start.7

commit v2 on v1

--- a/solution.py
+++ b/solution.py
@@ -1,9 +1,13 @@
 import jax
 import jax.numpy as jnp
 from jax import lax
+from jax.experimental import pallas as pl
+from jax.experimental.pallas import tpu as pltpu
 from jax.sharding import PartitionSpec as P
 
 NREG = 8
+GROUP = 16
+CHUNKS = 2
 
 
 def extended(value, sides, width):
@@ -68,6 +72,160 @@
     return result[..., 0]
 
 
+def plain_increment(
+    ens_coarse, col_interp, row_weights, ctrl_vec, band_loc, row_loc, level_loc, total_members
+):
+    fine_rows = row_weights.shape[1]
+    columns = band_loc.shape[0]
+    coarse_cols = jnp.einsum(
+        "tklic,jc->tklij", ens_coarse, col_interp, preferred_element_type=jnp.float32
+    ).astype(jnp.bfloat16)
+    stencil = row_matrix(row_weights, fine_rows, fine_rows // 2)
+    refined = jnp.einsum(
+        "tklij,ri->tkljr",
+        lax.all_to_all(coarse_cols, "tile", split_axis=4, concat_axis=3, tiled=True),
+        stencil,
+        preferred_element_type=jnp.float32,
+    ).astype(jnp.bfloat16)
+    member_fine = refined[0]
+    slot_term = member_fine * ctrl_vec[0][None]
+    projected = slot_term.astype(jnp.bfloat16)
+    if lax.axis_size("grp") > 1:
+        projected = lax.psum(projected, "grp")
+    padded = extended(projected, (("tile", 2),), columns)
+    banded = jnp.einsum(
+        "jq,klqr->kljr", band_loc, padded, preferred_element_type=jnp.float32
+    ).astype(jnp.bfloat16)
+    row_mixed = jnp.einsum(
+        "kljs,rs->kljr", banded, row_loc, preferred_element_type=jnp.float32
+    ).astype(jnp.bfloat16)
+    localized = jnp.einsum(
+        "lm,kmjr->kljr", level_loc, row_mixed, preferred_element_type=jnp.float32
+    ).astype(jnp.bfloat16)
+    return swap_add(
+        jnp.sum(member_fine.astype(jnp.float32) * localized.astype(jnp.float32), axis=0)
+    ) / (total_members - 1)
+
+
+def member_kernel(
+    before, own, after, ctrl, stencil, band, row_loc, level_loc, total, proj, fine, banded, mixed
+):
+    columns, levels, rows = total.shape
+    window = proj.shape[0]
+
+    @pl.when(pl.program_id(0) == 0)
+    def _():
+        total[...] = jnp.zeros_like(total)
+
+    for q in range(window):
+        source = (before, own, after)[q // columns]
+        refined = lax.dot_general(
+            source[0, q % columns],
+            stencil[...],
+            (((0,), (0,)), ((), ())),
+            preferred_element_type=jnp.float32,
+        ).astype(jnp.bfloat16)
+        if q // columns == 1:
+            fine[q % columns] = refined
+        proj[q] = (refined.astype(jnp.float32) * ctrl[q]).astype(jnp.bfloat16)
+    for pair in range(levels // (2 * GROUP)):
+        parts = []
+        for half in range(2):
+            start = (2 * pair + half) * GROUP
+            parts.append(proj[:, start : start + GROUP, :].reshape(window * GROUP, rows))
+        result = jnp.dot(
+            band[...], jnp.concatenate(parts, axis=1), preferred_element_type=jnp.float32
+        ).astype(jnp.bfloat16)
+        for half in range(2):
+            start = (2 * pair + half) * GROUP
+            banded[:, start : start + GROUP, :] = result[:, half * rows : (half + 1) * rows].reshape(
+                columns, GROUP, rows
+            )
+    mixed[...] = lax.dot_general(
+        banded[...].reshape(columns * levels, rows),
+        row_loc[...],
+        (((1,), (1,)), ((), ())),
+        preferred_element_type=jnp.float32,
+    ).astype(jnp.bfloat16)
+    for j in range(columns):
+        localized = jnp.dot(
+            level_loc[...],
+            mixed[j * levels : (j + 1) * levels, :],
+            preferred_element_type=jnp.float32,
+        )
+        total[j] += fine[j].astype(jnp.float32) * localized
+
+
+def member_sum(before, own, after, ctrl, stencil, band, row_loc, level_loc):
+    members, columns, coarse_rows, levels = own.shape
+    window, _, rows = ctrl.shape
+    block = pl.BlockSpec((1, columns, coarse_rows, levels), lambda k: (k, 0, 0, 0))
+
+    def whole(value):
+        return pl.BlockSpec(value.shape, lambda k: (0,) * value.ndim)
+
+    flops = 2 * members * levels * rows * (
+        window * coarse_rows + columns * (window * GROUP + rows + levels)
+    )
+    return pl.pallas_call(
+        member_kernel,
+        grid=(members,),
+        out_shape=jax.ShapeDtypeStruct((columns, levels, rows), jnp.float32),
+        in_specs=[block, block, block]
+        + [whole(value) for value in (ctrl, stencil, band, row_loc, level_loc)],
+        out_specs=pl.BlockSpec((columns, levels, rows), lambda k: (0, 0, 0)),
+        scratch_shapes=[
+            pltpu.VMEM((window, levels, rows), jnp.bfloat16),
+            pltpu.VMEM((columns, levels, rows), jnp.bfloat16),
+            pltpu.VMEM((columns, levels, rows), jnp.bfloat16),
+            pltpu.VMEM((columns * levels, rows), jnp.bfloat16),
+        ],
+        compiler_params=pltpu.CompilerParams(
+            dimension_semantics=("arbitrary",), vmem_limit_bytes=24 * 1024 * 1024
+        ),
+        cost_estimate=pl.CostEstimate(
+            flops=4 * flops, bytes_accessed=6 * own.size, transcendentals=0
+        ),
+    )(before, own, after, ctrl, stencil, band, row_loc, level_loc)
+
+
+def neighbours(value):
+    peers = lax.axis_size("tile")
+    up = [(i, (i + 1) % peers) for i in range(peers - 1)]
+    down = [(j, i) for i, j in up]
+    return lax.ppermute(value, "tile", up), lax.ppermute(value, "tile", down)
+
+
+def fused_increment(
+    ens_coarse, col_interp, row_weights, ctrl_vec, band_loc, row_loc, level_loc, total_members
+):
+    fine_rows = row_weights.shape[1]
+    stencil = row_matrix(row_weights, fine_rows, fine_rows // 2).T
+    band = jnp.kron(band_loc, jnp.eye(GROUP, dtype=jnp.bfloat16))
+    ctrl_own = jnp.swapaxes(ctrl_vec[0], 0, 1)
+    ctrl_before, ctrl_after = neighbours(ctrl_own)
+    ctrl = jnp.concatenate([ctrl_before, ctrl_own, ctrl_after], axis=0)
+    members = ens_coarse.shape[1]
+    chunks = CHUNKS if members % CHUNKS == 0 else 1
+    size = members // chunks
+    total = None
+    for chunk in range(chunks):
+        piece = ens_coarse[0, chunk * size : (chunk + 1) * size]
+        coarse_cols = jnp.einsum(
+            "klic,jc->jkil", piece, col_interp, preferred_element_type=jnp.float32
+        ).astype(jnp.bfloat16)
+        peers = lax.axis_size("tile")
+        columns = coarse_cols.shape[0] // peers
+        blocks = coarse_cols.reshape((peers, columns) + coarse_cols.shape[1:])
+        moved = lax.all_to_all(blocks, "tile", split_axis=0, concat_axis=0, tiled=True)
+        own = jnp.transpose(moved, (2, 1, 0, 3, 4))
+        own = own.reshape(size, columns, -1, own.shape[-1])
+        before, after = neighbours(own)
+        part = member_sum(before, own, after, ctrl, stencil, band, row_loc, level_loc)
+        total = part if total is None else total + part
+    return swap_add(jnp.swapaxes(total, 0, 1)) / (total_members - 1)
+
+
 def body(
     ens_coarse,
     col_interp,
@@ -81,8 +239,6 @@
     obs_prec,
     obs_region,
 ):
-    fine_rows = row_weights.shape[1]
-    columns = band_loc.shape[0]
     total_members = hx_pert.shape[1]
     observed = hx_pert[0]
     weighted = (observed * obs_prec[0][None, :]).astype(jnp.bfloat16)
@@ -96,34 +252,10 @@
     )
     sums = jnp.concatenate([gram_sums, right_side[:, :, None]], axis=2)
     sums = swap_add(lax.psum(sums, "grp") if lax.axis_size("grp") > 1 else sums)
-    coarse_cols = jnp.einsum(
-        "tklic,jc->tklij", ens_coarse, col_interp, preferred_element_type=jnp.float32
-    ).astype(jnp.bfloat16)
-    stencil = row_matrix(row_weights, fine_rows, fine_rows // 2)
-    refined = jnp.einsum(
-        "tklij,ri->tkljr",
-        lax.all_to_all(coarse_cols, "tile", split_axis=4, concat_axis=3, tiled=True),
-        stencil,
-        preferred_element_type=jnp.float32,
-    ).astype(jnp.bfloat16)
-    member_fine = refined[0]
-    slot_term = member_fine * ctrl_vec[0][None]
-    projected = slot_term.astype(jnp.bfloat16)
-    if lax.axis_size("grp") > 1:
-        projected = lax.psum(projected, "grp")
-    padded = extended(projected, (("tile", 2),), columns)
-    banded = jnp.einsum(
-        "jq,klqr->kljr", band_loc, padded, preferred_element_type=jnp.float32
-    ).astype(jnp.bfloat16)
-    row_mixed = jnp.einsum(
-        "kljs,rs->kljr", banded, row_loc, preferred_element_type=jnp.float32
-    ).astype(jnp.bfloat16)
-    localized = jnp.einsum(
-        "lm,kmjr->kljr", level_loc, row_mixed, preferred_element_type=jnp.float32
-    ).astype(jnp.bfloat16)
-    increment = swap_add(
-        jnp.sum(member_fine.astype(jnp.float32) * localized.astype(jnp.float32), axis=0)
-    ) / (total_members - 1)
+    plan = fused_increment if lax.axis_size("grp") == 1 else plain_increment
+    increment = plan(
+        ens_coarse, col_interp, row_weights, ctrl_vec, band_loc, row_loc, level_loc, total_members
+    )
     own_weights = solve_weights(sums[:, :, :total_members], sums[:, :, total_members])
     weights = collect(own_weights)
     return (increment[None], weights)

time: 461 us -> 296 us (0.64)
  waiting for transfers between devices: 288 us -> 128 us
  matrix products: 59.2 us -> 6.52 us
  Pallas kernels: 0 us -> 46.5 us
  other arithmetic: 76.2 us -> 58.6 us
  starting transfers between devices: 13.4 us -> 29.2 us
    ppermute x2 -> x6, waiting for transfers between devices: 165 us -> 31 us  [neighbours(): return (lax.ppermute(value, 'tile', up), lax.ppermute(value, 'tile', down))]
    dot_general x4 -> x2, matrix products: 57 us -> 4.36 us  [fused_increment(): jnp.einsum('klic,jc->jkil', piece, col_interp, preferred_element_type=jnp...]
    pallas_call x0 -> x2, Pallas kernels: none -> 46.5 us  [member_sum(): pl.pallas_call(member_kernel, grid=(members,), out_shape=jax.ShapeDtypeSt...]
    all_to_all x1 -> x2, waiting for transfers between devices: 114 us -> 92.9 us  [fused_increment(): lax.all_to_all(blocks, 'tile', split_axis=0, concat_axis=0, tiled=True)]
    concatenate x1, other arithmetic: 21.7 us -> 1.5 us  [fused_increment(): ctrl = jnp.concatenate([ctrl_before, ctrl_own, ctrl_after], axis=0)]
    ppermute x2 -> x6, starting transfers between devices: 4.5 us -> 15.3 us  [neighbours(): return (lax.ppermute(value, 'tile', up), lax.ppermute(value, 'tile', down))]
    convert_element_type x1 -> x0, local copies, waits for them, and re-layouts: 9.82 us -> none  [body(): coarse_cols = jnp.einsum('tklic,jc->tklij', ens_coarse, col_interp, prefe...]
    reshape x0 -> x2, local copies, waits for them, and re-layouts: none -> 9.78 us  [fused_increment(): blocks = coarse_cols.reshape((peers, columns) + coarse_cols.shape[1:])]
  transfers between devices with their start and end apart: 6 -> 11, of which waited for: 5 -> 4; matrix products, arithmetic and copies ran while one was open for 12% -> 27% of each run, Pallas kernels for 0% -> 8%
where the time goes in v2:
time: 296 us; the launch traced here: 294 us
  waiting for transfers between devices  128 us (43%)
  other arithmetic  58.6 us (20%)
  Pallas kernels  46.5 us (16%)
  starting transfers between devices  29.2 us (10%)
  local copies, waits for them, and re-layouts  23.9 us (8%)
  matrix products  6.52 us (2%)
    all_to_all x2, waiting for transfers between devices, fused_increment(): lax.all_to_all(blocks, 'tile', split_axis=0, concat_axis=0, tiled=True)  92.9 us
    pallas_call x2, Pallas kernels, member_sum(): pl.pallas_call(member_kernel, grid=(members,), out_shape=jax.ShapeDtypeSt...  46.5 us
    ppermute x6, waiting for transfers between devices, neighbours(): return (lax.ppermute(value, 'tile', up), lax.ppermute(value, 'tile', down))  31 us
    another operation x4, other arithmetic, solve_weights(): factor = jnp.linalg.cholesky(system)  29.5 us
    another operation x3, other arithmetic, solve_weights(): lax.linalg.triangular_solve(factor, halfway, left_side=True, lower=True,...  24.7 us
    ppermute x6, starting transfers between devices, neighbours(): return (lax.ppermute(value, 'tile', up), lax.ppermute(value, 'tile', down))  15.3 us
    all_to_all x2, starting transfers between devices, fused_increment(): lax.all_to_all(blocks, 'tile', split_axis=0, concat_axis=0, tiled=True)  11.3 us
    reshape x2, local copies, waits for them, and re-layouts, fused_increment(): blocks = coarse_cols.reshape((peers, columns) + coarse_cols.shape[1:])  9.78 us
  transfers between devices with their start and end apart: 11, of which 4 were waited for; matrix products, arithmetic and copies ran while one was open for 27% of the time, Pallas kernels for 8%

profile of v2, /device:TPU:14, one launch (start us, length us, event | category | flops | bytes accessed | tf_op | source)
XLA Modules:
  0.0 293.5 jit_solution(7241379773903900391)
XLA Ops:
  1.4 2.2 convert_bitcast_fusion
  3.5 4.9 %copy.39 = bf16[16,8,20,4,128]{4,3,1,2,0:T(4,128)(2,1)} copy(bf16[16,8,20,4,128]{4,1,0,3,2:T(8,128)(2,1)S(1)} %convert_bitcast_fusion) | data formatting | bytes 5242880 | tf_op jit(solution)/shard_map/reshape | solution.py:219
  8.4 6.2 %all-to-all-start.1 = ((bf16[16,8,20,4,128]{4,3,1,2,0:T(4,128)(2,1)}), bf16[16,8,20,4,128]{4,3,1,2,0:T(4,128)(2,1)S(1)}, u32[]{:S(2)}, u32[]{:S(2)}) async-start(bf16[16,8,20,4,128]{4,3,1,2,0:T(4,128)(2,1)} %copy.39), calls=%async_computation.1 | async-start | bytes 5242880 | tf_op jit(solution)/shard_map/all_to_all | solution.py:220
  14.7 2.2 convert_bitcast_fusion.1
  16.9 4.9 %copy.36 = bf16[16,8,20,4,128]{4,3,1,2,0:T(4,128)(2,1)} copy(bf16[16,8,20,4,128]{4,1,0,3,2:T(8,128)(2,1)S(1)} %convert_bitcast_fusion.1) | data formatting | bytes 5242880 | tf_op jit(solution)/shard_map/reshape | solution.py:219
  21.8 51.3 %all-to-all-done.1 = bf16[16,8,20,4,128]{4,3,1,2,0:T(4,128)(2,1)S(1)} async-done(((bf16[16,8,20,4,128]{4,3,1,2,0:T(4,128)(2,1)}), bf16[16,8,20,4,128]{4,3,1,2,0:T(4,128)(2,1)S(1)}, u32[]{:S(2)}, u32[]{:S(2)}) %all-to-all-start.1) | async-done | bytes 2621472 | tf_op jit(solution)/shard_map/all_to_all | solution.py:220
  73.1 1.5 copy-done.3
  74.6 5.1 %all-to-all-start = ((bf16[16,8,20,4,128]{4,3,1,2,0:T(4,128)(2,1)}), bf16[16,8,20,4,128]{4,3,1,2,0:T(4,128)(2,1)}, u32[]{:S(2)}, u32[]{:S(2)}) async-start(bf16[16,8,20,4,128]{4,3,1,2,0:T(4,128)(2,1)} %copy.36), calls=%async_computation | async-start | bytes 5242880 | tf_op jit(solution)/shard_map/all_to_all | solution.py:220
  84.2 1.9 collective-permute-start.2
  86.9 3.2 %copy.40 = bf16[20,8,16,4,128]{4,3,2,1,0:T(4,128)(2,1)S(1)} copy(bf16[20,8,16,4,128]{4,3,1,0,2:T(4,128)(2,1)} %bitcast.89) | data formatting | bytes 5242880 | tf_op jit(solution)/shard_map/transpose | solution.py:221
  90.1 3.5 %collective-permute-start.4 = (bf16[20,8,64,128]{3,2,1,0:T(8,128)(2,1)S(1)}, bf16[20,8,64,128]{3,2,1,0:T(8,128)(2,1)}, u32[]{:S(2)}, u32[]{:S(2)}) collective-permute-start(bf16[20,8,64,128]{3,2,1,0:T(8,128)(2,1)S(1)} %bitcast.86), channel_id=1, source_target_pairs={{0,2},{2,4},{4,6},{6,8},{8,10},{10,12},{12,14},{14,16},{16,18},{18... | collective-permute-start | bytes 7864328 | tf_op jit(solution)/shard_map/ppermute | solution.py:196
  93.6 2.3 collective-permute-start.5
  98.6 41.6 %all-to-all-done = bf16[16,8,20,4,128]{4,3,1,2,0:T(4,128)(2,1)} async-done(((bf16[16,8,20,4,128]{4,3,1,2,0:T(4,128)(2,1)}), bf16[16,8,20,4,128]{4,3,1,2,0:T(4,128)(2,1)}, u32[]{:S(2)}, u32[]{:S(2)}) %all-to-all-start) | async-done | bytes 2621472 | tf_op jit(solution)/shard_map/all_to_all | solution.py:220
  140.1 4.7 %copy.37 = bf16[20,8,16,4,128]{4,3,2,1,0:T(4,128)(2,1)} copy(bf16[20,8,16,4,128]{4,3,1,0,2:T(4,128)(2,1)} %bitcast.5) | data formatting | bytes 5242880 | tf_op jit(solution)/shard_map/transpose | solution.py:221
  144.9 2.7 collective-permute-start
  147.6 3.0 %collective-permute-start.1 = (bf16[20,8,64,128]{3,2,1,0:T(8,128)(2,1)}, bf16[20,8,64,128]{3,2,1,0:T(8,128)(2,1)}, u32[]{:S(2)}, u32[]{:S(2)}) collective-permute-start(bf16[20,8,64,128]{3,2,1,0:T(8,128)(2,1)} %bitcast.6.own), channel_id=1, source_target_pairs={{2,0},{4,2},{6,4},{8,6},{10,8},{12,10},{14,12},{16,14},{18,16},{20... | collective-permute-start | bytes 7864328 | tf_op jit(solution)/shard_map/ppermute | solution.py:196
  150.6 29.3 %custom-call.9 = f32[4,80,80]{2,1,0:T(8,128)S(1)} custom-call(f32[4,80,80]{2,1,0:T(8,128)S(1)} %fusion.22), custom_call_target="Cholesky" | custom-call | tf_op jit(solution)/shard_map/jit(cholesky)/cholesky | solution.py:67
  180.0 1.9 collective-permute-start.3
  182.1 24.6 %custom-call.10 = f32[4,1,80,80]{2,3,1,0:T(8,128)S(1)} custom-call(f32[4,1,80,80]{3,2,1,0:T(8,128)S(1)} %select_bitcast_fusion), custom_call_target="InvertDiagBlocksLowerTriangular" | custom-call | tf_op jit(solution)/shard_map/triangular_solve | solution.py:69
  207.0 31.0 %collective-permute-done.3 = f32[8,128,128]{2,1,0:T(8,128)} collective-permute-done((f32[8,128,128]{2,1,0:T(8,128)}, f32[8,128,128]{2,1,0:T(8,128)}, u32[]{:S(2)}, u32[]{:S(2)}) %collective-permute-start.3) | collective-permute-done | bytes 524320 | tf_op jit(solution)/shard_map/ppermute | solution.py:196
  238.0 1.5 pad_maximum_fusion.ctrl
  239.5 23.2 %shard_map.123 = f32[8,128,128]{2,1,0:T(8,128)S(1)} custom-call(bf16[20,8,64,128]{3,2,1,0:T(8,128)(2,1)} %collective-permute-done.4.before, bf16[20,8,64,128]{3,2,1,0:T(8,128)(2,1)S(1)} %bitcast.88, bf16[20,8,64,128]{3,2,1,0:T(8,128)(2,1)} %collective-permute-done.5.after, f32[24,128,128]{2,1,0:T(8,128)S(1)} %pad_maximum_fusion.ctrl, ...), custom_call_target="tpu_custom_call" | custom-call | flops 17448304640 | bytes 7864320 | tf_op jit(solution)/shard_map/pallas_call | solution.py:170
  262.7 23.3 %shard_map.122 = f32[8,128,128]{2,1,0:T(8,128)S(1)} custom-call(bf16[20,8,64,128]{3,2,1,0:T(8,128)(2,1)} %collective-permute-done.before, bf16[20,8,64,128]{3,2,1,0:T(8,128)(2,1)} %bitcast.6.own, bf16[20,8,64,128]{3,2,1,0:T(8,128)(2,1)} %collective-permute-done.1.after, f32[24,128,128]{2,1,0:T(8,128)S(1)} %pad_maximum_fusion.ctrl, ...), custom_call_target="tpu_custom_call" | custom-call | flops 17448304640 | bytes 7864320 | tf_op jit(solution)/shard_map/pallas_call | solution.py:170
  288.6 4.0 %collective-permute-done.8 = f32[4,80]{1,0:T(4,128)S(1)} collective-permute-done((f32[4,80]{1,0:T(4,128)S(1)}, f32[4,80]{1,0:T(4,128)S(1)}, u32[]{:S(2)}, u32[]{:S(2)}) %collective-permute-start.8) | collective-permute-done | bytes 1312 | tf_op jit(solution)/shard_map/ppermute | solution.py:47
  (71 shorter events, 12.6 us)
Async XLA Ops:
  8.4 64.6 %all-to-all-start.1 = ((bf16[16,8,20,4,128]{4,3,1,2,0:T(4,128)(2,1)}), bf16[16,8,20,4,128]{4,3,1,2,0:T(4,128)(2,1)S(1)}, u32[]{:S(2)}, u32[]{:S(2)}) async-start(bf16[16,8,20,4,128]{4,3,1,2,0:T(4,128)(2,1)} %copy.39), calls=%async_computation.1 | async-start | bytes 5242880 | tf_op jit(solution)/shard_map/all_to_all | solution.py:220
  21.7 57.9 %copy-start.7 = (bf16[1,80,2048]{2,1,0:T(8,128)(2,1)S(1)}, bf16[1,80,2048]{2,1,0:T(8,128)(2,1)}, u32[]{:S(2)}) copy-start(bf16[1,80,2048]{2,1,0:T(8,128)(2,1)} %param.18) | copy-start | bytes 983044
  21.7 57.9 %copy-start.8 = (s32[1,2048]{1,0:T(1,128)S(1)}, s32[1,2048]{1,0:T(1,128)}, u32[]{:S(2)}) copy-start(s32[1,2048]{1,0:T(1,128)} %param.21) | copy-start | bytes 24580
  21.7 57.9 %copy-start.9 = (f32[1,2048]{1,0:T(1,128)S(1)}, f32[1,2048]{1,0:T(1,128)}, u32[]{:S(2)}) copy-start(f32[1,2048]{1,0:T(1,128)} %param.20) | copy-start | bytes 24580
  21.8 57.9 %copy-start.13 = (f32[1,2048]{1,0:T(1,128)S(1)}, f32[1,2048]{1,0:T(1,128)}, u32[]{:S(2)}) copy-start(f32[1,2048]{1,0:T(1,128)} %param.19) | copy-start | bytes 24580
  73.1 1.5 copy-start.3
  74.6 65.5 %all-to-all-start = ((bf16[16,8,20,4,128]{4,3,1,2,0:T(4,128)(2,1)}), bf16[16,8,20,4,128]{4,3,1,2,0:T(4,128)(2,1)}, u32[]{:S(2)}, u32[]{:S(2)}) async-start(bf16[16,8,20,4,128]{4,3,1,2,0:T(4,128)(2,1)} %copy.36), calls=%async_computation | async-start | bytes 5242880 | tf_op jit(solution)/shard_map/all_to_all | solution.py:220
  80.2 3.2 %copy-start.5 = (f32[1,128,8,128]{3,2,1,0:T(8,128)S(1)}, f32[1,128,8,128]{3,2,1,0:T(8,128)}, u32[]{:S(2)}) copy-start(f32[1,128,8,128]{3,2,1,0:T(8,128)} %param.14) | copy-start | bytes 1572868
  80.2 6.7 %copy-start.12 = (bf16[3,128]{1,0:T(4,128)(2,1)S(1)}, bf16[3,128]{1,0:T(4,128)(2,1)}, u32[]{:S(2)}) copy-start(bf16[3,128]{1,0:T(4,128)(2,1)} %param.13) | copy-start | bytes 2308
  81.4 0.7 copy-start.4
  82.8 13.8 %collective-permute-start.7 = (f32[4,80,81]{1,2,0:T(8,128)}, f32[4,80,81]{1,2,0:T(8,128)}, u32[]{:S(2)}, u32[]{:S(2)}) collective-permute-start(f32[4,80,81]{1,2,0:T(8,128)} %fusion.16), channel_id=1, source_target_pairs={{0,1},{1,0},{2,3},{3,2},{4,5},{5,4},{6,7},{7,6},{8,9},{9,8},{10,11... | collective-permute-start | bytes 311048 | tf_op jit(solution)/shard_map/ppermute | solution.py:35
  84.2 95.8 %collective-permute-start.2 = (f32[8,128,128]{2,1,0:T(8,128)}, f32[8,128,128]{2,1,0:T(8,128)}, u32[]{:S(2)}, u32[]{:S(2)}) collective-permute-start(f32[8,128,128]{2,1,0:T(8,128)} %bitcast.85), channel_id=1, source_target_pairs={{0,2},{2,4},{4,6},{6,8},{8,10},{10,12},{12,14},{14,16},{16,18},{18... | collective-permute-start | bytes 1572872 | tf_op jit(solution)/shard_map/ppermute | solution.py:196
  86.8 9.0 %copy-start.11 = (bf16[8,24]{1,0:T(8,128)(2,1)S(1)}, bf16[8,24]{1,0:T(8,128)(2,1)}, u32[]{:S(2)}) copy-start(bf16[8,24]{1,0:T(8,128)(2,1)} %param.15) | copy-start | bytes 1156
  90.1 149.4 %collective-permute-start.4 = (bf16[20,8,64,128]{3,2,1,0:T(8,128)(2,1)S(1)}, bf16[20,8,64,128]{3,2,1,0:T(8,128)(2,1)}, u32[]{:S(2)}, u32[]{:S(2)}) collective-permute-start(bf16[20,8,64,128]{3,2,1,0:T(8,128)(2,1)S(1)} %bitcast.86), channel_id=1, source_target_pairs={{0,2},{2,4},{4,6},{6,8},{8,10},{10,12},{12,14},{14,16},{16,18},{18... | collective-permute-start | bytes 7864328 | tf_op jit(solution)/shard_map/ppermute | solution.py:196
  93.6 145.9 %collective-permute-start.5 = (bf16[20,8,64,128]{3,2,1,0:T(8,128)(2,1)S(1)}, bf16[20,8,64,128]{3,2,1,0:T(8,128)(2,1)}, u32[]{:S(2)}, u32[]{:S(2)}) collective-permute-start(bf16[20,8,64,128]{3,2,1,0:T(8,128)(2,1)S(1)} %bitcast.87), channel_id=1, source_target_pairs={{2,0},{4,2},{6,4},{8,6},{10,8},{12,10},{14,12},{16,14},{18,16},{20... | collective-permute-start | bytes 7864328 | tf_op jit(solution)/shard_map/ppermute | solution.py:196
  140.1 10.4 %copy-start.6 = (f32[80,80]{0,1:T(8,128)S(1)}, f32[80,80]{0,1:T(8,128)}, u32[]{:S(2)}) copy-start(f32[80,80]{0,1:T(8,128)} %copy.42) | copy-start | bytes 76804
  144.9 94.6 %copy-start.1 = (bf16[128,128]{1,0:T(8,128)(2,1)S(1)}, bf16[128,128]{1,0:T(8,128)(2,1)}, u32[]{:S(2)}) copy-start(bf16[128,128]{1,0:T(8,128)(2,1)} %row_loc.3) | copy-start | bytes 98308
  144.9 94.6 %copy-start.2 = (bf16[128,128]{1,0:T(8,128)(2,1)S(1)}, bf16[128,128]{1,0:T(8,128)(2,1)}, u32[]{:S(2)}) copy-start(bf16[128,128]{1,0:T(8,128)(2,1)} %level_loc.3) | copy-start | bytes 98308
  144.9 117.9 %collective-permute-start = (bf16[20,8,64,128]{3,2,1,0:T(8,128)(2,1)}, bf16[20,8,64,128]{3,2,1,0:T(8,128)(2,1)}, u32[]{:S(2)}, u32[]{:S(2)}) collective-permute-start(bf16[20,8,64,128]{3,2,1,0:T(8,128)(2,1)} %bitcast.6.own), channel_id=1, source_target_pairs={{0,2},{2,4},{4,6},{6,8},{8,10},{10,12},{12,14},{14,16},{16,18},{18... | collective-permute-start | bytes 7864328 | tf_op jit(solution)/shard_map/ppermute | solution.py:196
  147.6 115.1 %collective-permute-start.1 = (bf16[20,8,64,128]{3,2,1,0:T(8,128)(2,1)}, bf16[20,8,64,128]{3,2,1,0:T(8,128)(2,1)}, u32[]{:S(2)}, u32[]{:S(2)}) collective-permute-start(bf16[20,8,64,128]{3,2,1,0:T(8,128)(2,1)} %bitcast.6.own), channel_id=1, source_target_pairs={{2,0},{4,2},{6,4},{8,6},{10,8},{12,10},{14,12},{16,14},{18,16},{20... | collective-permute-start | bytes 7864328 | tf_op jit(solution)/shard_map/ppermute | solution.py:196
  180.0 58.0 %collective-permute-start.3 = (f32[8,128,128]{2,1,0:T(8,128)}, f32[8,128,128]{2,1,0:T(8,128)}, u32[]{:S(2)}, u32[]{:S(2)}) collective-permute-start(f32[8,128,128]{2,1,0:T(8,128)} %bitcast.85), channel_id=1, source_target_pairs={{2,0},{4,2},{6,4},{8,6},{10,8},{12,10},{14,12},{16,14},{18,16},{20... | collective-permute-start | bytes 1572872 | tf_op jit(solution)/shard_map/ppermute | solution.py:196
  286.1 6.5 %collective-permute-start.6 = (f32[64,8,128]{2,0,1:T(8,128)S(1)}, f32[64,8,128]{2,0,1:T(8,128)S(1)}, u32[]{:S(2)}, u32[]{:S(2)}) collective-permute-start(f32[64,8,128]{2,0,1:T(8,128)S(1)} %dynamic-slice_bitcast_fusion), channel_id=1, source_target_pairs={{0,1},{1,0},{2,3},{3,2},{4,5},{5,4},{6,7},{7,6},{8,9},{9,8},{10,11... | collective-permute-start | bytes 786440 | tf_op jit(solution)/shard_map/ppermute | solution.py:35
  287.9 4.7 %collective-permute-start.8 = (f32[4,80]{1,0:T(4,128)S(1)}, f32[4,80]{1,0:T(4,128)S(1)}, u32[]{:S(2)}, u32[]{:S(2)}) collective-permute-start(f32[4,80]{1,0:T(4,128)S(1)} %bitcast.92), channel_id=1, source_target_pairs={{0,1},{1,0},{2,3},{3,2},{4,5},{5,4},{6,7},{7,6},{8,9},{9,8},{10,11... | collective-permute-start | bytes 3848 | tf_op jit(solution)/shard_map/ppermute | solution.py:47
  292.6 0.9 copy-start.10
  (1 other events, 0.7 us)
